TPU v7x, 32 devices: a whole 2x2x4 slice. The times are simulated.
32 devices in a mesh: row: 8 (over z, y), col: 4 (over x, core).
Axes of the slice: x: 2, y: 2, z: 4, core: 2. Of those that a mesh axis runs over, the one named last changes fastest.
Arguments:
- rhs: float32 [2, 8, 64, 512], P(None, 'row'), may hold values from -6 to 6
- inverse_t: float32 [2, 8, 512, 512], P(None, 'row', None, 'col'), may hold values from -1 to 2, as said below
- u_factors: bfloat16 [2, 8, 4, 4, 32, 512], P(None, 'row', None, 'col'), may hold values from -0.14941406 to 0.14941406
- v_factors: bfloat16 [2, 8, 4, 4, 32, 512], P(None, 'row', None, 'col'), may hold values from -0.14941406 to 0.14941406
- tile_ranks: int32 [2, 8, 4, 4], P(None, 'row', None, 'col'), may hold values from 8 to 32
Outputs:
- solved: float32 [2, 8, 64, 512], P(None, 'row')
Inputs may be any that keep to these rules, and one draw needn't show every extreme that they name: `inverse_t`: each transposed inverse is nonsingular and of order one.
All inputs are finite; a program needn't handle non-finite values.
Results may differ from a plain program's by a relative error of at most 0.004.
Values may be sent and summed in bfloat16 or wider, within the bound.
No kernel may reach another device: no remote copies, remote signals or barrier semaphores. Data moves between devices by JAX's collectives and lax.ppermute only.
A program may use at most 64 MiB of HBM per device.

v0:
```python
import jax
import jax.numpy as jnp
from jax import lax
from jax.sharding import PartitionSpec as P


def broadcast(block, axis, source):
    block = jnp.where(lax.axis_index(axis) == source, block, jnp.zeros_like(block))
    return lax.psum(block, axis)


def pick(array, index, axis):
    return lax.dynamic_index_in_dim(array, index, axis, keepdims=False)


def on_device(rhs, inverse_t, u_factors, v_factors, tile_ranks):
    rhs_here = rhs[:, 0]
    slots = rhs_here.shape[0]
    rank_width = u_factors.shape[4]
    n_row = lax.axis_size("row")
    n_col = lax.axis_size("col")
    blocks = slots * n_row
    my_row = lax.axis_index("row")
    my_col = lax.axis_index("col")
    global_rows = jnp.arange(slots, dtype=jnp.int32) * n_row + my_row
    rank_cols = lax.broadcasted_iota(jnp.int32, (1, 1, rank_width), 2)
    start = jnp.zeros(rhs_here.shape, jnp.float32)

    def apply_update(totals, full, u_col, v_col, ranks, active):
        seg_b = full.astype(jnp.bfloat16)
        proj = jnp.einsum("rb,akb->ark", seg_b, v_col, preferred_element_type=jnp.float32)
        keep = (rank_cols < ranks[:, None, None]) & active[:, None, None]
        proj_b = jnp.where(keep, proj, 0.0).astype(jnp.bfloat16)
        update = jnp.einsum("ark,akb->arb", proj_b, u_col, preferred_element_type=jnp.float32)
        return totals + update

    inverse_here = inverse_t[:, 0]
    u_here = u_factors[:, 0, :, 0]
    v_here = v_factors[:, 0, :, 0]
    ranks_here = tile_ranks[:, 0, :, 0]

    def step(k, carry):
        totals, solved = carry
        k_slot = k // n_row
        k_row = k % n_row
        c_slot = k // n_col
        c_dev = k % n_col
        summed = lax.psum(pick(totals, k_slot, 0).astype(jnp.bfloat16), "col").astype(jnp.float32)
        segment = pick(rhs_here, k_slot, 0) - summed
        piece = jnp.dot(
            segment,
            pick(inverse_here, k_slot, 0),
            precision=lax.Precision.HIGHEST,
            preferred_element_type=jnp.float32,
        )
        spread = broadcast(piece, "row", k_row)
        full = lax.all_gather(spread, "col", axis=1, tiled=True)
        previous = pick(solved, k_slot, 0)
        solved = lax.dynamic_update_index_in_dim(
            solved, jnp.where(my_row == k_row, full, previous), k_slot, 0
        )
        u_col = pick(u_here, c_slot, 1)
        v_col = pick(v_here, c_slot, 1)
        ranks = pick(ranks_here, c_slot, 1)
        active = (global_rows > k) & (my_col == c_dev)
        totals = apply_update(totals, full, u_col, v_col, ranks, active)
        return (totals, solved)

    totals, solved = lax.fori_loop(0, blocks, step, (start, start))
    return solved[:, None]


def solution(mesh):
    in_specs = (
        P(None, "row", None, None),
        P(None, "row", None, "col"),
        P(None, "row", None, "col", None, None),
        P(None, "row", None, "col", None, None),
        P(None, "row", None, "col"),
    )
    out_specs = P(None, "row", None, None)
    return jax.shard_map(
        on_device, mesh=mesh, in_specs=in_specs, out_specs=out_specs, check_vma=False
    )
```

profile of v0, /device:TPU:0, one launch (start us, length us, event | category | flops | bytes accessed | tf_op | source)
XLA Modules:
  0.0 1234.3 jit_solution(4183829090954470033)
XLA Ops:
  9.3 1217.8 %while.21 = (s32[]{:T(128)}, f32[2,64,512]{2,1,0:T(8,128)S(1)}, f32[2,64,512]{2,1,0:T(8,128)S(1)}, s32[2,4]{0,1:T(4,128)S(1)}, s32[]{:T(128)}, /*index=5*/bf16[2...) while((s32[]{:T(128)}, f32[2,64,512]{2,1,0:T(8,128)S(1)}, ...), condition=%wide.region_3.4_spmd.clone.clone.clone, body=%wide.region_0.3_spmd.clone.clone.clone.sunk | while | flops 59039912 | bytes 3215025 | solution.py:69
  10.2 36.5 %all-reduce.2.cloned.1.call-done = bf16[64,512]{1,0:T(8,128)(2,1)} async-done(((bf16[64,512]{1,0:T(8,128)(2,1)}), bf16[64,512]{1,0:T(8,128)(2,1)}) %all-reduce.2.cloned.1.call-update) | async-done | bytes 65552 | tf_op jit(solution)/shard_map/while/body/eval_jaxpr/psum | solution.py:48
  47.8 37.1 %psum.39 = f32[64,128]{1,0:T(8,128)S(1)} all-reduce(f32[64,128]{1,0:T(8,128)S(1)} %convolution_select_fusion.3), channel_id=1, replica_groups=mesh['row'=8,'col'=4] {'row'}, use_global_device_ids=true, to_apply=%region_2.2 | all-reduce | flops 8192 | bytes 65536 | tf_op jit(solution)/shard_map/while/body/eval_jaxpr/psum | solution.py:9
  92.5 30.0 %all-reduce.2.cloned.1.call-done = bf16[64,512]{1,0:T(8,128)(2,1)} async-done(((bf16[64,512]{1,0:T(8,128)(2,1)}), bf16[64,512]{1,0:T(8,128)(2,1)}) %all-reduce.2.cloned.1.call-update) | async-done | bytes 65552 | tf_op jit(solution)/shard_map/while/body/eval_jaxpr/psum | solution.py:48
  123.7 37.1 %psum.39 = f32[64,128]{1,0:T(8,128)S(1)} all-reduce(f32[64,128]{1,0:T(8,128)S(1)} %convolution_select_fusion.3), channel_id=1, replica_groups=mesh['row'=8,'col'=4] {'row'}, use_global_device_ids=true, to_apply=%region_2.2 | all-reduce | flops 8192 | bytes 65536 | tf_op jit(solution)/shard_map/while/body/eval_jaxpr/psum | solution.py:9
  168.4 30.0 %all-reduce.2.cloned.1.call-done = bf16[64,512]{1,0:T(8,128)(2,1)} async-done(((bf16[64,512]{1,0:T(8,128)(2,1)}), bf16[64,512]{1,0:T(8,128)(2,1)}) %all-reduce.2.cloned.1.call-update) | async-done | bytes 65552 | tf_op jit(solution)/shard_map/while/body/eval_jaxpr/psum | solution.py:48
  199.5 37.1 %psum.39 = f32[64,128]{1,0:T(8,128)S(1)} all-reduce(f32[64,128]{1,0:T(8,128)S(1)} %convolution_select_fusion.3), channel_id=1, replica_groups=mesh['row'=8,'col'=4] {'row'}, use_global_device_ids=true, to_apply=%region_2.2 | all-reduce | flops 8192 | bytes 65536 | tf_op jit(solution)/shard_map/while/body/eval_jaxpr/psum | solution.py:9
  275.1 37.1 %psum.39 = f32[64,128]{1,0:T(8,128)S(1)} all-reduce(f32[64,128]{1,0:T(8,128)S(1)} %convolution_select_fusion.3), channel_id=1, replica_groups=mesh['row'=8,'col'=4] {'row'}, use_global_device_ids=true, to_apply=%region_2.2 | all-reduce | flops 8192 | bytes 65536 | tf_op jit(solution)/shard_map/while/body/eval_jaxpr/psum | solution.py:9
  350.6 37.1 %psum.39 = f32[64,128]{1,0:T(8,128)S(1)} all-reduce(f32[64,128]{1,0:T(8,128)S(1)} %convolution_select_fusion.3), channel_id=1, replica_groups=mesh['row'=8,'col'=4] {'row'}, use_global_device_ids=true, to_apply=%region_2.2 | all-reduce | flops 8192 | bytes 65536 | tf_op jit(solution)/shard_map/while/body/eval_jaxpr/psum | solution.py:9
  426.2 37.1 %psum.39 = f32[64,128]{1,0:T(8,128)S(1)} all-reduce(f32[64,128]{1,0:T(8,128)S(1)} %convolution_select_fusion.3), channel_id=1, replica_groups=mesh['row'=8,'col'=4] {'row'}, use_global_device_ids=true, to_apply=%region_2.2 | all-reduce | flops 8192 | bytes 65536 | tf_op jit(solution)/shard_map/while/body/eval_jaxpr/psum | solution.py:9
  470.9 30.0 %all-reduce.2.cloned.1.call-done = bf16[64,512]{1,0:T(8,128)(2,1)} async-done(((bf16[64,512]{1,0:T(8,128)(2,1)}), bf16[64,512]{1,0:T(8,128)(2,1)}) %all-reduce.2.cloned.1.call-update) | async-done | bytes 65552 | tf_op jit(solution)/shard_map/while/body/eval_jaxpr/psum | solution.py:48
  502.1 37.1 %psum.39 = f32[64,128]{1,0:T(8,128)S(1)} all-reduce(f32[64,128]{1,0:T(8,128)S(1)} %convolution_select_fusion.3), channel_id=1, replica_groups=mesh['row'=8,'col'=4] {'row'}, use_global_device_ids=true, to_apply=%region_2.2 | all-reduce | flops 8192 | bytes 65536 | tf_op jit(solution)/shard_map/while/body/eval_jaxpr/psum | solution.py:9
  546.8 30.0 %all-reduce.2.cloned.1.call-done = bf16[64,512]{1,0:T(8,128)(2,1)} async-done(((bf16[64,512]{1,0:T(8,128)(2,1)}), bf16[64,512]{1,0:T(8,128)(2,1)}) %all-reduce.2.cloned.1.call-update) | async-done | bytes 65552 | tf_op jit(solution)/shard_map/while/body/eval_jaxpr/psum | solution.py:48
  577.9 37.1 %psum.39 = f32[64,128]{1,0:T(8,128)S(1)} all-reduce(f32[64,128]{1,0:T(8,128)S(1)} %convolution_select_fusion.3), channel_id=1, replica_groups=mesh['row'=8,'col'=4] {'row'}, use_global_device_ids=true, to_apply=%region_2.2 | all-reduce | flops 8192 | bytes 65536 | tf_op jit(solution)/shard_map/while/body/eval_jaxpr/psum | solution.py:9
  622.6 30.0 %all-reduce.2.cloned.1.call-done = bf16[64,512]{1,0:T(8,128)(2,1)} async-done(((bf16[64,512]{1,0:T(8,128)(2,1)}), bf16[64,512]{1,0:T(8,128)(2,1)}) %all-reduce.2.cloned.1.call-update) | async-done | bytes 65552 | tf_op jit(solution)/shard_map/while/body/eval_jaxpr/psum | solution.py:48
  653.8 37.1 %psum.39 = f32[64,128]{1,0:T(8,128)S(1)} all-reduce(f32[64,128]{1,0:T(8,128)S(1)} %convolution_select_fusion.3), channel_id=1, replica_groups=mesh['row'=8,'col'=4] {'row'}, use_global_device_ids=true, to_apply=%region_2.2 | all-reduce | flops 8192 | bytes 65536 | tf_op jit(solution)/shard_map/while/body/eval_jaxpr/psum | solution.py:9
  729.4 37.1 %psum.39 = f32[64,128]{1,0:T(8,128)S(1)} all-reduce(f32[64,128]{1,0:T(8,128)S(1)} %convolution_select_fusion.3), channel_id=1, replica_groups=mesh['row'=8,'col'=4] {'row'}, use_global_device_ids=true, to_apply=%region_2.2 | all-reduce | flops 8192 | bytes 65536 | tf_op jit(solution)/shard_map/while/body/eval_jaxpr/psum | solution.py:9
  805.2 37.1 %psum.39 = f32[64,128]{1,0:T(8,128)S(1)} all-reduce(f32[64,128]{1,0:T(8,128)S(1)} %convolution_select_fusion.3), channel_id=1, replica_groups=mesh['row'=8,'col'=4] {'row'}, use_global_device_ids=true, to_apply=%region_2.2 | all-reduce | flops 8192 | bytes 65536 | tf_op jit(solution)/shard_map/while/body/eval_jaxpr/psum | solution.py:9
  880.8 37.1 %psum.39 = f32[64,128]{1,0:T(8,128)S(1)} all-reduce(f32[64,128]{1,0:T(8,128)S(1)} %convolution_select_fusion.3), channel_id=1, replica_groups=mesh['row'=8,'col'=4] {'row'}, use_global_device_ids=true, to_apply=%region_2.2 | all-reduce | flops 8192 | bytes 65536 | tf_op jit(solution)/shard_map/while/body/eval_jaxpr/psum | solution.py:9
  925.5 30.0 %all-reduce.2.cloned.1.call-done = bf16[64,512]{1,0:T(8,128)(2,1)} async-done(((bf16[64,512]{1,0:T(8,128)(2,1)}), bf16[64,512]{1,0:T(8,128)(2,1)}) %all-reduce.2.cloned.1.call-update) | async-done | bytes 65552 | tf_op jit(solution)/shard_map/while/body/eval_jaxpr/psum | solution.py:48
  956.6 37.1 %psum.39 = f32[64,128]{1,0:T(8,128)S(1)} all-reduce(f32[64,128]{1,0:T(8,128)S(1)} %convolution_select_fusion.3), channel_id=1, replica_groups=mesh['row'=8,'col'=4] {'row'}, use_global_device_ids=true, to_apply=%region_2.2 | all-reduce | flops 8192 | bytes 65536 | tf_op jit(solution)/shard_map/while/body/eval_jaxpr/psum | solution.py:9
  1032.2 37.1 %psum.39 = f32[64,128]{1,0:T(8,128)S(1)} all-reduce(f32[64,128]{1,0:T(8,128)S(1)} %convolution_select_fusion.3), channel_id=1, replica_groups=mesh['row'=8,'col'=4] {'row'}, use_global_device_ids=true, to_apply=%region_2.2 | all-reduce | flops 8192 | bytes 65536 | tf_op jit(solution)/shard_map/while/body/eval_jaxpr/psum | solution.py:9
  1107.7 37.1 %psum.39 = f32[64,128]{1,0:T(8,128)S(1)} all-reduce(f32[64,128]{1,0:T(8,128)S(1)} %convolution_select_fusion.3), channel_id=1, replica_groups=mesh['row'=8,'col'=4] {'row'}, use_global_device_ids=true, to_apply=%region_2.2 | all-reduce | flops 8192 | bytes 65536 | tf_op jit(solution)/shard_map/while/body/eval_jaxpr/psum | solution.py:9
  1183.3 37.1 %psum.39 = f32[64,128]{1,0:T(8,128)S(1)} all-reduce(f32[64,128]{1,0:T(8,128)S(1)} %convolution_select_fusion.3), channel_id=1, replica_groups=mesh['row'=8,'col'=4] {'row'}, use_global_device_ids=true, to_apply=%region_2.2 | all-reduce | flops 8192 | bytes 65536 | tf_op jit(solution)/shard_map/while/body/eval_jaxpr/psum | solution.py:9
  (211 shorter events, 409.0 us)
Async XLA Ops:
  6.5 1.8 copy-start
  8.3 1.0 copy-start.2
  9.3 37.4 %all-reduce.2.cloned.1.call-start = ((), (), s32[]{:S(2)}) async-start(), calls=%async_computation | async-start | bytes 131072 | tf_op jit(solution)/shard_map/while/body/eval_jaxpr/psum | solution.py:48
  91.6 30.9 %all-reduce.2.cloned.1.call-start = ((), (), s32[]{:S(2)}) async-start(), calls=%async_computation | async-start | bytes 131072 | tf_op jit(solution)/shard_map/while/body/eval_jaxpr/psum | solution.py:48
  167.5 30.9 %all-reduce.2.cloned.1.call-start = ((), (), s32[]{:S(2)}) async-start(), calls=%async_computation | async-start | bytes 131072 | tf_op jit(solution)/shard_map/while/body/eval_jaxpr/psum | solution.py:48
  243.3 30.6 %all-reduce.2.cloned.1.call-start = ((), (), s32[]{:S(2)}) async-start(), calls=%async_computation | async-start | bytes 131072 | tf_op jit(solution)/shard_map/while/body/eval_jaxpr/psum | solution.py:48
  318.9 30.6 %all-reduce.2.cloned.1.call-start = ((), (), s32[]{:S(2)}) async-start(), calls=%async_computation | async-start | bytes 131072 | tf_op jit(solution)/shard_map/while/body/eval_jaxpr/psum | solution.py:48
  394.4 30.6 %all-reduce.2.cloned.1.call-start = ((), (), s32[]{:S(2)}) async-start(), calls=%async_computation | async-start | bytes 131072 | tf_op jit(solution)/shard_map/while/body/eval_jaxpr/psum | solution.py:48
  470.0 30.9 %all-reduce.2.cloned.1.call-start = ((), (), s32[]{:S(2)}) async-start(), calls=%async_computation | async-start | bytes 131072 | tf_op jit(solution)/shard_map/while/body/eval_jaxpr/psum | solution.py:48
  545.8 30.9 %all-reduce.2.cloned.1.call-start = ((), (), s32[]{:S(2)}) async-start(), calls=%async_computation | async-start | bytes 131072 | tf_op jit(solution)/shard_map/while/body/eval_jaxpr/psum | solution.py:48
  621.7 30.9 %all-reduce.2.cloned.1.call-start = ((), (), s32[]{:S(2)}) async-start(), calls=%async_computation | async-start | bytes 131072 | tf_op jit(solution)/shard_map/while/body/eval_jaxpr/psum | solution.py:48
  697.6 30.6 %all-reduce.2.cloned.1.call-start = ((), (), s32[]{:S(2)}) async-start(), calls=%async_computation | async-start | bytes 131072 | tf_op jit(solution)/shard_map/while/body/eval_jaxpr/psum | solution.py:48
  773.1 30.9 %all-reduce.2.cloned.1.call-start = ((), (), s32[]{:S(2)}) async-start(), calls=%async_computation | async-start | bytes 131072 | tf_op jit(solution)/shard_map/while/body/eval_jaxpr/psum | solution.py:48
  849.0 30.6 %all-reduce.2.cloned.1.call-start = ((), (), s32[]{:S(2)}) async-start(), calls=%async_computation | async-start | bytes 131072 | tf_op jit(solution)/shard_map/while/body/eval_jaxpr/psum | solution.py:48
  924.6 30.9 %all-reduce.2.cloned.1.call-start = ((), (), s32[]{:S(2)}) async-start(), calls=%async_computation | async-start | bytes 131072 | tf_op jit(solution)/shard_map/while/body/eval_jaxpr/psum | solution.py:48
  1000.4 30.6 %all-reduce.2.cloned.1.call-start = ((), (), s32[]{:S(2)}) async-start(), calls=%async_computation | async-start | bytes 131072 | tf_op jit(solution)/shard_map/while/body/eval_jaxpr/psum | solution.py:48
  1076.0 30.6 %all-reduce.2.cloned.1.call-start = ((), (), s32[]{:S(2)}) async-start(), calls=%async_computation | async-start | bytes 131072 | tf_op jit(solution)/shard_map/while/body/eval_jaxpr/psum | solution.py:48
  1151.5 30.6 %all-reduce.2.cloned.1.call-start = ((), (), s32[]{:S(2)}) async-start(), calls=%async_computation | async-start | bytes 131072 | tf_op jit(solution)/shard_map/while/body/eval_jaxpr/psum | solution.py:48
  1227.1 0.7 copy-start.1
Sparse Core Ops, SparseCore 0:
  12.4 34.2 all-reduce.1
  94.7 27.7 all-reduce.1
  170.6 27.7 all-reduce.1
  246.1 27.7 all-reduce.1
  321.7 27.7 all-reduce.1
  397.2 27.7 all-reduce.1
  473.1 27.7 all-reduce.1
  549.0 27.7 all-reduce.1
  624.8 27.7 all-reduce.1
  700.4 27.7 all-reduce.1
  776.3 27.7 all-reduce.1
  851.8 27.7 all-reduce.1
  927.7 27.7 all-reduce.1
  1003.2 27.7 all-reduce.1
  1078.8 27.7 all-reduce.1
  1154.3 27.7 all-reduce.1
where the time goes:
time: 1240 us; the launch traced here: 1230 us
  blocking collectives  680 us (55%)
  waiting for transfers between devices  484 us (39%)
  matrix products  38 us (3%)
  local copies, waits for them, and re-layouts  14 us (1%)
  between operations  13.1 us (1%)
    psum x16, blocking collectives, broadcast(): return lax.psum(block, axis)  593 us
    psum x16, waiting for transfers between devices, step(): lax.psum(pick(totals, k_slot, 0).astype(jnp.bfloat16), 'col')  484 us
    all_gather x16, blocking collectives, step(): full = lax.all_gather(spread, 'col', axis=1, tiled=True)  86.4 us
  transfers between devices with their start and end apart: 16, of which 16 were waited for; matrix products, arithmetic and copies ran while one was open for 0% of the time, Pallas kernels for 0%

commit v1 on v0

--- a/solution.py
+++ b/solution.py
@@ -6,7 +6,12 @@
 
 def broadcast(block, axis, source):
     block = jnp.where(lax.axis_index(axis) == source, block, jnp.zeros_like(block))
-    return lax.psum(block, axis)
+
+    def _step_on_arrays(content, axis_tag):
+        even = jnp.sum(lax.all_gather(content, axis_tag), axis=0)
+        return even
+
+    return _step_on_arrays(block, axis)
 
 
 def pick(array, index, axis):

time: 1240 us -> 1190 us (0.960)
  blocking collectives: 680 us -> 582 us
  waiting for transfers between devices: 484 us -> 539 us
    psum x16 -> x0, blocking collectives: 593 us -> none  [broadcast(): return lax.psum(block, axis)]
    all_gather x0 -> x16, blocking collectives: none -> 495 us  [_step_on_arrays(): even = jnp.sum(lax.all_gather(content, axis_tag), axis=0)]
    psum x16, waiting for transfers between devices: 484 us -> 539 us  [step(): lax.psum(pick(totals, k_slot, 0).astype(jnp.bfloat16), 'col')]
where the time goes in v1:
time: 1190 us
  blocking collectives  582 us (49%)
  waiting for transfers between devices  539 us (45%)
  matrix products  38 us (3%)
  local copies, waits for them, and re-layouts  14 us (1%)
  between operations  13.1 us (1%)
    psum x16, waiting for transfers between devices, step(): lax.psum(pick(totals, k_slot, 0).astype(jnp.bfloat16), 'col')  539 us
    all_gather x16, blocking collectives, _step_on_arrays(): even = jnp.sum(lax.all_gather(content, axis_tag), axis=0)  495 us
    all_gather x16, blocking collectives, step(): full = lax.all_gather(spread, 'col', axis=1, tiled=True)  86.7 us
  transfers between devices with their start and end apart: 16, of which 16 were waited for; matrix products, arithmetic and copies ran while one was open for 0% of the time, Pallas kernels for 0%

profile of v1, /device:TPU:0, one launch (start us, length us, event | category | flops | bytes accessed | tf_op | source)
XLA Modules:
  0.0 1190.7 jit_solution(5614252504671415684)
XLA Ops:
  9.3 1174.2 %while.21 = (s32[]{:T(128)}, f32[2,64,512]{2,1,0:T(8,128)S(1)}, f32[2,64,512]{2,1,0:T(8,128)S(1)}, s32[2,4]{0,1:T(4,128)S(1)}, s32[]{:T(128)}, /*index=5*/bf16[2...) while((s32[]{:T(128)}, f32[2,64,512]{2,1,0:T(8,128)S(1)}, ...), condition=%wide.region_3.4_spmd.clone.clone.clone, body=%wide.region_0.3_spmd.clone.clone.clone.sunk | while | flops 59089064 | bytes 3739325 | solution.py:74
  10.2 36.5 %all-reduce.2.cloned.1.call-done = bf16[64,512]{1,0:T(8,128)(2,1)} async-done(((bf16[64,512]{1,0:T(8,128)(2,1)}), bf16[64,512]{1,0:T(8,128)(2,1)}) %all-reduce.2.cloned.1.call-update) | async-done | bytes 65552 | tf_op jit(solution)/shard_map/while/body/eval_jaxpr/psum | solution.py:53
  86.4 33.7 %all-reduce.2.cloned.1.call-done = bf16[64,512]{1,0:T(8,128)(2,1)} async-done(((bf16[64,512]{1,0:T(8,128)(2,1)}), bf16[64,512]{1,0:T(8,128)(2,1)}) %all-reduce.2.cloned.1.call-update) | async-done | bytes 65552 | tf_op jit(solution)/shard_map/while/body/eval_jaxpr/psum | solution.py:53
  121.2 30.9 %all-gather.5 = f32[512,128]{1,0:T(8,128)S(1)} all-gather(f32[64,128]{1,0:T(8,128)S(1)} %convolution_select_fusion.3), channel_id=2, replica_groups=mesh['row'=8,'col'=4] {'row'}, dimensions={0}, use_global_device_ids=true | all-gather | bytes 294912 | tf_op jit(solution)/shard_map/while/body/eval_jaxpr/all_gather | solution.py:11
  159.8 33.6 %all-reduce.2.cloned.1.call-done = bf16[64,512]{1,0:T(8,128)(2,1)} async-done(((bf16[64,512]{1,0:T(8,128)(2,1)}), bf16[64,512]{1,0:T(8,128)(2,1)}) %all-reduce.2.cloned.1.call-update) | async-done | bytes 65552 | tf_op jit(solution)/shard_map/while/body/eval_jaxpr/psum | solution.py:53
  194.5 30.9 %all-gather.5 = f32[512,128]{1,0:T(8,128)S(1)} all-gather(f32[64,128]{1,0:T(8,128)S(1)} %convolution_select_fusion.3), channel_id=2, replica_groups=mesh['row'=8,'col'=4] {'row'}, dimensions={0}, use_global_device_ids=true | all-gather | bytes 294912 | tf_op jit(solution)/shard_map/while/body/eval_jaxpr/all_gather | solution.py:11
  233.1 33.3 %all-reduce.2.cloned.1.call-done = bf16[64,512]{1,0:T(8,128)(2,1)} async-done(((bf16[64,512]{1,0:T(8,128)(2,1)}), bf16[64,512]{1,0:T(8,128)(2,1)}) %all-reduce.2.cloned.1.call-update) | async-done | bytes 65552 | tf_op jit(solution)/shard_map/while/body/eval_jaxpr/psum | solution.py:53
  267.6 30.9 %all-gather.5 = f32[512,128]{1,0:T(8,128)S(1)} all-gather(f32[64,128]{1,0:T(8,128)S(1)} %convolution_select_fusion.3), channel_id=2, replica_groups=mesh['row'=8,'col'=4] {'row'}, dimensions={0}, use_global_device_ids=true | all-gather | bytes 294912 | tf_op jit(solution)/shard_map/while/body/eval_jaxpr/all_gather | solution.py:11
  306.2 33.3 %all-reduce.2.cloned.1.call-done = bf16[64,512]{1,0:T(8,128)(2,1)} async-done(((bf16[64,512]{1,0:T(8,128)(2,1)}), bf16[64,512]{1,0:T(8,128)(2,1)}) %all-reduce.2.cloned.1.call-update) | async-done | bytes 65552 | tf_op jit(solution)/shard_map/while/body/eval_jaxpr/psum | solution.py:53
  340.6 30.9 %all-gather.5 = f32[512,128]{1,0:T(8,128)S(1)} all-gather(f32[64,128]{1,0:T(8,128)S(1)} %convolution_select_fusion.3), channel_id=2, replica_groups=mesh['row'=8,'col'=4] {'row'}, dimensions={0}, use_global_device_ids=true | all-gather | bytes 294912 | tf_op jit(solution)/shard_map/while/body/eval_jaxpr/all_gather | solution.py:11
  379.2 33.3 %all-reduce.2.cloned.1.call-done = bf16[64,512]{1,0:T(8,128)(2,1)} async-done(((bf16[64,512]{1,0:T(8,128)(2,1)}), bf16[64,512]{1,0:T(8,128)(2,1)}) %all-reduce.2.cloned.1.call-update) | async-done | bytes 65552 | tf_op jit(solution)/shard_map/while/body/eval_jaxpr/psum | solution.py:53
  452.3 33.7 %all-reduce.2.cloned.1.call-done = bf16[64,512]{1,0:T(8,128)(2,1)} async-done(((bf16[64,512]{1,0:T(8,128)(2,1)}), bf16[64,512]{1,0:T(8,128)(2,1)}) %all-reduce.2.cloned.1.call-update) | async-done | bytes 65552 | tf_op jit(solution)/shard_map/while/body/eval_jaxpr/psum | solution.py:53
  487.1 30.9 %all-gather.5 = f32[512,128]{1,0:T(8,128)S(1)} all-gather(f32[64,128]{1,0:T(8,128)S(1)} %convolution_select_fusion.3), channel_id=2, replica_groups=mesh['row'=8,'col'=4] {'row'}, dimensions={0}, use_global_device_ids=true | all-gather | bytes 294912 | tf_op jit(solution)/shard_map/while/body/eval_jaxpr/all_gather | solution.py:11
  525.7 33.7 %all-reduce.2.cloned.1.call-done = bf16[64,512]{1,0:T(8,128)(2,1)} async-done(((bf16[64,512]{1,0:T(8,128)(2,1)}), bf16[64,512]{1,0:T(8,128)(2,1)}) %all-reduce.2.cloned.1.call-update) | async-done | bytes 65552 | tf_op jit(solution)/shard_map/while/body/eval_jaxpr/psum | solution.py:53
  560.4 30.9 %all-gather.5 = f32[512,128]{1,0:T(8,128)S(1)} all-gather(f32[64,128]{1,0:T(8,128)S(1)} %convolution_select_fusion.3), channel_id=2, replica_groups=mesh['row'=8,'col'=4] {'row'}, dimensions={0}, use_global_device_ids=true | all-gather | bytes 294912 | tf_op jit(solution)/shard_map/while/body/eval_jaxpr/all_gather | solution.py:11
  599.0 33.7 %all-reduce.2.cloned.1.call-done = bf16[64,512]{1,0:T(8,128)(2,1)} async-done(((bf16[64,512]{1,0:T(8,128)(2,1)}), bf16[64,512]{1,0:T(8,128)(2,1)}) %all-reduce.2.cloned.1.call-update) | async-done | bytes 65552 | tf_op jit(solution)/shard_map/while/body/eval_jaxpr/psum | solution.py:53
  672.4 33.3 %all-reduce.2.cloned.1.call-done = bf16[64,512]{1,0:T(8,128)(2,1)} async-done(((bf16[64,512]{1,0:T(8,128)(2,1)}), bf16[64,512]{1,0:T(8,128)(2,1)}) %all-reduce.2.cloned.1.call-update) | async-done | bytes 65552 | tf_op jit(solution)/shard_map/while/body/eval_jaxpr/psum | solution.py:53
  745.5 33.7 %all-reduce.2.cloned.1.call-done = bf16[64,512]{1,0:T(8,128)(2,1)} async-done(((bf16[64,512]{1,0:T(8,128)(2,1)}), bf16[64,512]{1,0:T(8,128)(2,1)}) %all-reduce.2.cloned.1.call-update) | async-done | bytes 65552 | tf_op jit(solution)/shard_map/while/body/eval_jaxpr/psum | solution.py:53
  818.9 33.3 %all-reduce.2.cloned.1.call-done = bf16[64,512]{1,0:T(8,128)(2,1)} async-done(((bf16[64,512]{1,0:T(8,128)(2,1)}), bf16[64,512]{1,0:T(8,128)(2,1)}) %all-reduce.2.cloned.1.call-update) | async-done | bytes 65552 | tf_op jit(solution)/shard_map/while/body/eval_jaxpr/psum | solution.py:53
  891.9 33.7 %all-reduce.2.cloned.1.call-done = bf16[64,512]{1,0:T(8,128)(2,1)} async-done(((bf16[64,512]{1,0:T(8,128)(2,1)}), bf16[64,512]{1,0:T(8,128)(2,1)}) %all-reduce.2.cloned.1.call-update) | async-done | bytes 65552 | tf_op jit(solution)/shard_map/while/body/eval_jaxpr/psum | solution.py:53
  965.3 33.3 %all-reduce.2.cloned.1.call-done = bf16[64,512]{1,0:T(8,128)(2,1)} async-done(((bf16[64,512]{1,0:T(8,128)(2,1)}), bf16[64,512]{1,0:T(8,128)(2,1)}) %all-reduce.2.cloned.1.call-update) | async-done | bytes 65552 | tf_op jit(solution)/shard_map/while/body/eval_jaxpr/psum | solution.py:53
  999.8 30.9 %all-gather.5 = f32[512,128]{1,0:T(8,128)S(1)} all-gather(f32[64,128]{1,0:T(8,128)S(1)} %convolution_select_fusion.3), channel_id=2, replica_groups=mesh['row'=8,'col'=4] {'row'}, dimensions={0}, use_global_device_ids=true | all-gather | bytes 294912 | tf_op jit(solution)/shard_map/while/body/eval_jaxpr/all_gather | solution.py:11
  1038.3 33.3 %all-reduce.2.cloned.1.call-done = bf16[64,512]{1,0:T(8,128)(2,1)} async-done(((bf16[64,512]{1,0:T(8,128)(2,1)}), bf16[64,512]{1,0:T(8,128)(2,1)}) %all-reduce.2.cloned.1.call-update) | async-done | bytes 65552 | tf_op jit(solution)/shard_map/while/body/eval_jaxpr/psum | solution.py:53
  1111.4 33.3 %all-reduce.2.cloned.1.call-done = bf16[64,512]{1,0:T(8,128)(2,1)} async-done(((bf16[64,512]{1,0:T(8,128)(2,1)}), bf16[64,512]{1,0:T(8,128)(2,1)}) %all-reduce.2.cloned.1.call-update) | async-done | bytes 65552 | tf_op jit(solution)/shard_map/while/body/eval_jaxpr/psum | solution.py:53
  (227 shorter events, 420.3 us)
Async XLA Ops:
  6.5 1.8 copy-start
  8.3 1.0 copy-start.2
  9.3 37.4 %all-reduce.2.cloned.1.call-start = ((), (), s32[]{:S(2)}) async-start(), calls=%async_computation | async-start | bytes 131072 | tf_op jit(solution)/shard_map/while/body/eval_jaxpr/psum | solution.py:53
  85.5 34.6 %all-reduce.2.cloned.1.call-start = ((), (), s32[]{:S(2)}) async-start(), calls=%async_computation | async-start | bytes 131072 | tf_op jit(solution)/shard_map/while/body/eval_jaxpr/psum | solution.py:53
  158.8 34.6 %all-reduce.2.cloned.1.call-start = ((), (), s32[]{:S(2)}) async-start(), calls=%async_computation | async-start | bytes 131072 | tf_op jit(solution)/shard_map/while/body/eval_jaxpr/psum | solution.py:53
  232.2 34.2 %all-reduce.2.cloned.1.call-start = ((), (), s32[]{:S(2)}) async-start(), calls=%async_computation | async-start | bytes 131072 | tf_op jit(solution)/shard_map/while/body/eval_jaxpr/psum | solution.py:53
  305.2 34.3 %all-reduce.2.cloned.1.call-start = ((), (), s32[]{:S(2)}) async-start(), calls=%async_computation | async-start | bytes 131072 | tf_op jit(solution)/shard_map/while/body/eval_jaxpr/psum | solution.py:53
  378.3 34.2 %all-reduce.2.cloned.1.call-start = ((), (), s32[]{:S(2)}) async-start(), calls=%async_computation | async-start | bytes 131072 | tf_op jit(solution)/shard_map/while/body/eval_jaxpr/psum | solution.py:53
  451.3 34.6 %all-reduce.2.cloned.1.call-start = ((), (), s32[]{:S(2)}) async-start(), calls=%async_computation | async-start | bytes 131072 | tf_op jit(solution)/shard_map/while/body/eval_jaxpr/psum | solution.py:53
  524.7 34.6 %all-reduce.2.cloned.1.call-start = ((), (), s32[]{:S(2)}) async-start(), calls=%async_computation | async-start | bytes 131072 | tf_op jit(solution)/shard_map/while/body/eval_jaxpr/psum | solution.py:53
  598.1 34.6 %all-reduce.2.cloned.1.call-start = ((), (), s32[]{:S(2)}) async-start(), calls=%async_computation | async-start | bytes 131072 | tf_op jit(solution)/shard_map/while/body/eval_jaxpr/psum | solution.py:53
  671.5 34.3 %all-reduce.2.cloned.1.call-start = ((), (), s32[]{:S(2)}) async-start(), calls=%async_computation | async-start | bytes 131072 | tf_op jit(solution)/shard_map/while/body/eval_jaxpr/psum | solution.py:53
  744.6 34.6 %all-reduce.2.cloned.1.call-start = ((), (), s32[]{:S(2)}) async-start(), calls=%async_computation | async-start | bytes 131072 | tf_op jit(solution)/shard_map/while/body/eval_jaxpr/psum | solution.py:53
  817.9 34.2 %all-reduce.2.cloned.1.call-start = ((), (), s32[]{:S(2)}) async-start(), calls=%async_computation | async-start | bytes 131072 | tf_op jit(solution)/shard_map/while/body/eval_jaxpr/psum | solution.py:53
  891.0 34.6 %all-reduce.2.cloned.1.call-start = ((), (), s32[]{:S(2)}) async-start(), calls=%async_computation | async-start | bytes 131072 | tf_op jit(solution)/shard_map/while/body/eval_jaxpr/psum | solution.py:53
  964.4 34.2 %all-reduce.2.cloned.1.call-start = ((), (), s32[]{:S(2)}) async-start(), calls=%async_computation | async-start | bytes 131072 | tf_op jit(solution)/shard_map/while/body/eval_jaxpr/psum | solution.py:53
  1037.4 34.3 %all-reduce.2.cloned.1.call-start = ((), (), s32[]{:S(2)}) async-start(), calls=%async_computation | async-start | bytes 131072 | tf_op jit(solution)/shard_map/while/body/eval_jaxpr/psum | solution.py:53
  1110.5 34.2 %all-reduce.2.cloned.1.call-start = ((), (), s32[]{:S(2)}) async-start(), calls=%async_computation | async-start | bytes 131072 | tf_op jit(solution)/shard_map/while/body/eval_jaxpr/psum | solution.py:53
  1183.5 0.7 copy-start.1
Sparse Core Ops, SparseCore 0:
  12.4 34.2 all-reduce.1
  88.6 31.4 all-reduce.1
  162.0 31.3 all-reduce.1
  235.0 31.3 all-reduce.1
  308.1 31.3 all-reduce.1
  381.1 31.3 all-reduce.1
  454.5 31.4 all-reduce.1
  527.8 31.4 all-reduce.1
  601.2 31.4 all-reduce.1
  674.3 31.4 all-reduce.1
  747.7 31.4 all-reduce.1
  820.7 31.3 all-reduce.1
  894.1 31.4 all-reduce.1
  967.2 31.3 all-reduce.1
  1040.2 31.3 all-reduce.1
  1113.3 31.3 all-reduce.1
